TPU v7x, 512 devices: a whole 4x8x8 slice. The times are simulated.
512 devices in a mesh: row: 16 (over z, core), col: 4 (over x), depth: 8 (over y).
Axes of the slice: x: 4, y: 8, z: 8, core: 2. Of those that a mesh axis runs over, the one named last changes fastest.
Arguments:
- intersection_re: bfloat16 [8, 4096, 4096], P('depth', ('row', 'col')), may hold values from -1 to 1, as said below
- intersection_im: bfloat16 [8, 4096, 4096], P('depth', ('row', 'col')), may hold values from -1 to 1, as said below
- weights: float32 [8], replicated, may hold values from 0.5 to 2
- shells: int32 [8, 3], replicated, may hold values from -2 to 2
- rotation: bfloat16 [4096, 4096], P(('row', 'col')), may hold values from -6 to 6
Outputs:
- updated: float32 [4096, 4096], P(('row', 'col'), 'depth')
Inputs may be any that keep to these rules, and one draw needn't show every extreme that they name: `intersection_re`: diagonal entries lie in 0.5 to 1. `intersection_im`: diagonal entries lie in -0.6 to 0.6.
All inputs are finite; a program needn't handle non-finite values.
Results may differ from a plain program's by a relative error of at most 0.035.
Values may be sent and summed in bfloat16 or wider, within the bound.
No kernel may reach another device: no remote copies, remote signals or barrier semaphores. Data moves between devices by JAX's collectives and lax.ppermute only.
A program may use at most 64 MiB of HBM per device.

v0:
```python
import math
import jax
import jax.numpy as jnp
from jax import lax
from jax.sharding import PartitionSpec as P

TERMS = 8
LATTICE = 0.25


def from_everyone(shard, axis):
    copies = jnp.broadcast_to(shard, (lax.axis_size(axis), *shard.shape))
    return lax.all_to_all(copies, axis, split_axis=0, concat_axis=0, tiled=True)


def in_order(parts, dim):
    dims = list(parts.shape[1:])
    dims[dim] *= parts.shape[0]
    return jnp.moveaxis(parts, 0, dim).reshape(dims)


def gather_directly(shard, axis, dim):
    parts = from_everyone(shard, axis)
    return in_order(parts, dim)


def over_copies(shard, axis):
    everything = from_everyone(shard, axis)
    return jnp.sum(everything, axis=0)


def cut_along(shard, dim, devices):
    before, after = (shard.shape[:dim], shard.shape[dim + 1 :])
    return jnp.moveaxis(shard.reshape(*before, devices, -1, *after), dim, 0)


def sum_at_owner(shard, axis, dim):
    parts = cut_along(shard, dim, lax.axis_size(axis))
    arrived = lax.all_to_all(parts, axis, split_axis=0, concat_axis=0, tiled=True)
    return arrived.sum(axis=0)


def per_device(intersection_re, intersection_im, weights, shells, rotation):
    shells_here = intersection_re.shape[0]
    slab_rows = intersection_re.shape[1]
    width = intersection_re.shape[2]
    position = lax.axis_index(("row", "col"))
    layer_index = lax.axis_index("depth")
    depth_count = lax.axis_size("depth")
    block_re = lax.dynamic_slice_in_dim(intersection_re, position * slab_rows, slab_rows, 2)
    block_im = lax.dynamic_slice_in_dim(intersection_im, position * slab_rows, slab_rows, 2)
    diag_piece = jnp.stack(
        [jnp.diagonal(block_re, axis1=1, axis2=2), jnp.diagonal(block_im, axis1=1, axis2=2)], 1
    )
    first_shell = layer_index * shells_here
    own_weights = lax.dynamic_slice_in_dim(weights, first_shell, shells_here, 0)
    own_vectors = (
        lax.dynamic_slice_in_dim(shells, first_shell, shells_here, 0).astype(jnp.float32) * LATTICE
    )
    diagonals = gather_directly(diag_piece, ("row", "col"), 2).astype(jnp.float32)
    diag_re = diagonals[:, 0]
    diag_im = diagonals[:, 1]
    phase_own = jnp.arctan2(diag_im, diag_re)
    partial_centre = -jnp.einsum("bk,bn->kn", own_weights[:, None] * own_vectors, phase_own)
    centre = over_copies(partial_centre, "depth")
    spread = phase_own + jnp.einsum("bk,kn->bn", own_vectors, centre)
    modulus = diag_re * diag_re + diag_im * diag_im
    values_re = intersection_re.astype(jnp.float32)
    values_im = intersection_im.astype(jnp.float32)
    terms = values_re * diag_re[:, None, :] + values_im * diag_im[:, None, :]
    terms = (
        terms
        - spread[:, None, :]
        * (values_im * diag_re[:, None, :] - values_re * diag_im[:, None, :])
        / modulus[:, None, :]
    )
    local_sum = jnp.sum(own_weights[:, None, None] * terms, 0)
    factor = 1.25 / math.sqrt(depth_count * shells_here)
    slab_cols = width // depth_count
    mirrored = lax.all_to_all(local_sum, ("row", "col"), split_axis=1, concat_axis=0, tiled=True).T
    operator_rows = sum_at_owner(local_sum - mirrored, "depth", 1) * factor
    operator_piece = operator_rows.astype(jnp.bfloat16)
    operator_cols = lax.all_gather(operator_piece, ("row", "col"), axis=0, tiled=True)
    accum = lax.dynamic_slice_in_dim(rotation, layer_index * slab_cols, slab_cols, 1).astype(
        jnp.float32
    )
    product = jnp.dot(rotation, operator_cols, preferred_element_type=jnp.float32)
    for order in range(1, TERMS):
        series_term = (product / order).astype(jnp.bfloat16)
        accum = accum + series_term.astype(jnp.float32)
        if order + 1 < TERMS:
            piece = gather_directly(series_term, "depth", 1)
            matching = lax.slice_in_dim(operator_cols, 0, piece.shape[1], axis=0)
            product = jnp.zeros_like(accum) + jnp.dot(
                piece, matching, preferred_element_type=jnp.float32
            )
    return accum


def solution(mesh):
    in_specs = (
        P("depth", ("row", "col"), None),
        P("depth", ("row", "col"), None),
        P(),
        P(),
        P(("row", "col"), None),
    )
    out_specs = P(("row", "col"), "depth")
    return jax.shard_map(
        per_device, mesh=mesh, in_specs=in_specs, out_specs=out_specs, check_vma=False
    )
```

profile of v0, /device:TPU:8, one launch (start us, length us, event | category | flops | bytes accessed | tf_op | source)
XLA Modules:
  0.0 354.2 jit_solution(16714782614347129712)
XLA Ops:
  6.6 0.9 dynamic-slice_bitcast_fusion
  7.5 0.9 gather_fusion.1
  8.3 0.9 gather_fusion
  9.2 0.6 broadcast_in_dim.34
  9.9 13.8 %all-to-all-start = ((bf16[64,1,2,64]{3,2,1,0:T(2,128)(2,1)}), bf16[64,1,2,64]{3,2,1,0:T(2,128)(2,1)S(1)}, u32[]{:S(2)}, u32[]{:S(2)}) async-start(bf16[64,1,2,64]{3,2,1,0:T(2,128)(2,1)} %broadcast_in_dim.34), calls=%async_computation | async-start | bytes 65536 | tf_op jit(solution)/shard_map/all_to_all | solution.py:13
  23.7 0.0 all-gather.2.cloned.1.call-start
  23.7 1.3 dynamic_slice.16
  25.7 0.9 multiply_reduce_fusion.1
  26.6 6.6 %all-to-all-done = bf16[64,1,2,64]{3,2,1,0:T(2,128)(2,1)S(1)} async-done(((bf16[64,1,2,64]{3,2,1,0:T(2,128)(2,1)}), bf16[64,1,2,64]{3,2,1,0:T(2,128)(2,1)S(1)}, u32[]{:S(2)}, u32[]{:S(2)}) %all-to-all-start) | async-done | bytes 16416 | tf_op jit(solution)/shard_map/all_to_all | solution.py:13
  33.3 0.1 reshape.91
  33.4 0.2 fusion.17
  33.7 0.1 multiply_negate_fusion
  33.7 0.1 broadcast_in_dim.35
  33.8 23.1 %all_to_all.64 = f32[8,3,4096]{2,1,0:T(4,128)S(1)} all-to-all(f32[8,3,4096]{2,1,0:T(4,128)S(1)} %broadcast_in_dim.35), channel_id=1, replica_groups=mesh['row'=16,'col'=4,'depth'=8] {'depth'}, dimensions={0} | all-to-all | bytes 786432 | tf_op jit(solution)/shard_map/all_to_all | solution.py:13
  56.9 0.1 reduce_sum.24
  57.0 0.1 fusion.15
  57.2 1.1 fusion.11
  58.3 2.2 all_to_all.43
  60.5 2.8 copy.56
  63.3 2.3 reshape.115
  65.6 33.6 %all_to_all.65 = f32[64,1,4096]{2,1,0:T(1,128)S(1)} all-to-all(f32[64,1,4096]{2,1,0:T(1,128)} %reshape.115), channel_id=1, replica_groups=mesh['row'=16,'col'=4,'depth'=8] {'row','col'}, dimensions={0} | all-to-all | bytes 2097152 | tf_op jit(solution)/shard_map/all_to_all | solution.py:80
  99.2 0.5 broadcast.60
  99.7 4.5 %reduce.4 = f32[64,4096]{1,0:T(8,128)} reduce(f32[64,1,4096]{2,1,0:T(1,128)S(1)} %all_to_all.65, f32[]{:T(128)} %broadcast.60), dimensions={1}, to_apply=%all_to_all.44.reduce_sub_computation | reduce | bytes 2097156 | tf_op jit(solution)/shard_map/all_to_all | solution.py:80
  104.2 2.0 reshape.116
  106.2 1.6 copy.39
  107.8 1.3 bitcast_subtract_fusion
  109.1 0.6 copy.54
  109.7 0.6 copy.40
  110.4 30.6 %all_to_all.66 = f32[8,64,512]{2,1,0:T(8,128)S(1)} all-to-all(f32[8,64,512]{2,1,0:T(8,128)S(1)} %copy.40), channel_id=1, replica_groups=mesh['row'=16,'col'=4,'depth'=8] {'depth'}, dimensions={0} | all-to-all | bytes 2097152 | tf_op jit(solution)/shard_map/all_to_all | solution.py:39
  140.9 0.1 reduce_sum.26
  141.0 0.6 multiply_convert_fusion
  141.7 0.0 all-gather.2.cloned.1.call-update
  141.7 78.4 %all-gather.2.cloned.1.call-done = bf16[4096,512]{1,0:T(8,128)(2,1)} async-done(((bf16[64,512]{1,0:T(8,128)(2,1)}), bf16[4096,512]{1,0:T(8,128)(2,1)}) %all-gather.2.cloned.1.call-update) | async-done | bytes 4194320 | tf_op jit(solution)/shard_map/all_gather | solution.py:83
  220.1 3.2 fusion.8
  223.3 23.5 %all_to_all.67 = bf16[8,64,512]{2,1,0:T(8,128)(2,1)S(1)} all-to-all(bf16[8,64,512]{2,1,0:T(8,128)(2,1)S(1)} %broadcast_in_dim.36), channel_id=1, replica_groups=mesh['row'=16,'col'=4,'depth'=8] {'depth'}, dimensions={0} | all-to-all | bytes 1048576 | tf_op jit(solution)/shard_map/all_to_all | solution.py:13
  246.9 0.8 fusion
  247.8 19.7 %all_to_all.68 = bf16[8,64,512]{2,1,0:T(8,128)(2,1)S(1)} all-to-all(bf16[8,64,512]{2,1,0:T(8,128)(2,1)S(1)} %broadcast_in_dim.37), channel_id=1, replica_groups=mesh['row'=16,'col'=4,'depth'=8] {'depth'}, dimensions={0} | all-to-all | bytes 1048576 | tf_op jit(solution)/shard_map/all_to_all | solution.py:13
  267.6 0.8 fusion.1
  268.5 18.5 %all_to_all.69 = bf16[8,64,512]{2,1,0:T(8,128)(2,1)S(1)} all-to-all(bf16[8,64,512]{2,1,0:T(8,128)(2,1)S(1)} %broadcast_in_dim.38), channel_id=1, replica_groups=mesh['row'=16,'col'=4,'depth'=8] {'depth'}, dimensions={0} | all-to-all | bytes 1048576 | tf_op jit(solution)/shard_map/all_to_all | solution.py:13
  287.0 0.8 fusion.2
  287.9 17.6 %all_to_all.70 = bf16[8,64,512]{2,1,0:T(8,128)(2,1)S(1)} all-to-all(bf16[8,64,512]{2,1,0:T(8,128)(2,1)S(1)} %broadcast_in_dim.39), channel_id=1, replica_groups=mesh['row'=16,'col'=4,'depth'=8] {'depth'}, dimensions={0} | all-to-all | bytes 1048576 | tf_op jit(solution)/shard_map/all_to_all | solution.py:13
  305.6 0.8 fusion.3
  306.5 17.6 %all_to_all.71 = bf16[8,64,512]{2,1,0:T(8,128)(2,1)S(1)} all-to-all(bf16[8,64,512]{2,1,0:T(8,128)(2,1)S(1)} %broadcast_in_dim.40), channel_id=1, replica_groups=mesh['row'=16,'col'=4,'depth'=8] {'depth'}, dimensions={0} | all-to-all | bytes 1048576 | tf_op jit(solution)/shard_map/all_to_all | solution.py:13
  324.2 0.8 fusion.4
  325.0 0.8 broadcast_in_dim.41
  325.8 4.9 %all-to-all-start.9 = ((bf16[8,64,512]{2,1,0:T(8,128)(2,1)}), bf16[8,64,512]{2,1,0:T(8,128)(2,1)S(1)}, u32[]{:S(2)}, u32[]{:S(2)}) async-start(bf16[8,64,512]{2,1,0:T(8,128)(2,1)} %broadcast_in_dim.41), calls=%async_computation.9 | async-start | bytes 1048576 | tf_op jit(solution)/shard_map/all_to_all | solution.py:13
  330.7 13.0 %all-to-all-done.9 = bf16[8,64,512]{2,1,0:T(8,128)(2,1)S(1)} async-done(((bf16[8,64,512]{2,1,0:T(8,128)(2,1)}), bf16[8,64,512]{2,1,0:T(8,128)(2,1)S(1)}, u32[]{:S(2)}, u32[]{:S(2)}) %all-to-all-start.9) | async-done | bytes 524320 | tf_op jit(solution)/shard_map/all_to_all | solution.py:13
  343.7 3.7 %fusion.7 = f32[64,512]{1,0:T(8,128)} fusion(bf16[64,4096]{1,0:T(8,128)(2,1)S(1)} %bitcast.88, bf16[4096,512]{1,0:T(8,128)(2,1)} %all-gather.2.cloned.1.call-done, bf16[64,512]{1,0:T(8,128)(2,1)S(1)} %fusion.4, bf16[64,512]{1,0:T(8,128)(2,1)S(1)} %fusion.3, bf16[64,512]{1,0:T(8,128)(2,1)S(1)} %fusion.2, bf16[64,512]{1,0:T(8,128)(2,1)S(1)} %fusion.1, ...), kind=kOutput, calls=%fused_computation.19 | convolution fusion | flops 268992512 | bytes 5308420 | tf_op jit(solution)/shard_map/dot_general | solution.py:94
  (24 shorter events, 0.5 us)
Async XLA Ops:
  6.5 50.7 %copy-start.3 = (bf16[1,64,4096]{2,1,0:T(8,128)(2,1)S(1)}, bf16[1,64,4096]{2,1,0:T(8,128)(2,1)}, u32[]{:S(2)}) copy-start(bf16[1,64,4096]{2,1,0:T(8,128)(2,1)} %param.6) | copy-start | bytes 1572868
  6.5 50.7 %copy-start.2 = (bf16[1,64,4096]{2,1,0:T(8,128)(2,1)S(1)}, bf16[1,64,4096]{2,1,0:T(8,128)(2,1)}, u32[]{:S(2)}) copy-start(bf16[1,64,4096]{2,1,0:T(8,128)(2,1)} %param.5) | copy-start | bytes 1572868
  9.9 23.4 %all-to-all-start = ((bf16[64,1,2,64]{3,2,1,0:T(2,128)(2,1)}), bf16[64,1,2,64]{3,2,1,0:T(2,128)(2,1)S(1)}, u32[]{:S(2)}, u32[]{:S(2)}) async-start(bf16[64,1,2,64]{3,2,1,0:T(2,128)(2,1)} %broadcast_in_dim.34), calls=%async_computation | async-start | bytes 65536 | tf_op jit(solution)/shard_map/all_to_all | solution.py:13
  23.7 196.4 %all-gather.2.cloned.1.call-start = ((), (), s32[]{:S(2)}) async-start(), calls=%async_computation.10 | async-start | bytes 4259840 | tf_op jit(solution)/shard_map/all_gather | solution.py:83
  109.1 111.0 %copy-start.1 = (bf16[64,4096]{1,0:T(8,128)(2,1)S(1)}, bf16[64,4096]{1,0:T(8,128)(2,1)}, u32[]{:S(2)}) copy-start(bf16[64,4096]{1,0:T(8,128)(2,1)} %param.9) | copy-start | bytes 1572868
  220.1 26.8 %copy-start = (bf16[4096,512]{1,0:T(8,128)(2,1)S(1)}, bf16[4096,512]{1,0:T(8,128)(2,1)}, u32[]{:S(2)}) copy-start(bf16[4096,512]{1,0:T(8,128)(2,1)} %all-gather.2.cloned.1.call-done) | copy-start | bytes 12582916
  325.8 17.8 %all-to-all-start.9 = ((bf16[8,64,512]{2,1,0:T(8,128)(2,1)}), bf16[8,64,512]{2,1,0:T(8,128)(2,1)S(1)}, u32[]{:S(2)}, u32[]{:S(2)}) async-start(bf16[8,64,512]{2,1,0:T(8,128)(2,1)} %broadcast_in_dim.41), calls=%async_computation.9 | async-start | bytes 1048576 | tf_op jit(solution)/shard_map/all_to_all | solution.py:13
Sparse Core Ops, SparseCore 0:
  141.8 78.2 all-gather.1
where the time goes:
time: 355 us; the launch traced here: 354 us
  blocking collectives  184 us (52%)
  waiting for transfers between devices  98 us (28%)
  local copies, waits for them, and re-layouts  18.7 us (5%)
  starting transfers between devices  18.7 us (5%)
  between operations  14.4 us (4%)
  matrix products  11.2 us (3%)
  other arithmetic  9.01 us (3%)
    all_to_all x6, blocking collectives, from_everyone(): return lax.all_to_all(copies, axis, split_axis=0, concat_axis=0, tiled=True)  120 us
    all_gather x1, waiting for transfers between devices, per_device(): lax.all_gather(operator_piece, ('row', 'col'), axis=0, tiled=True)  78.4 us
    all_to_all x1, blocking collectives, per_device(): lax.all_to_all(local_sum, ('row', 'col'), split_axis=1, concat_axis=0, ti...  33.6 us
    all_to_all x1, blocking collectives, sum_at_owner(): lax.all_to_all(parts, axis, split_axis=0, concat_axis=0, tiled=True)  30.6 us
    all_to_all x2, waiting for transfers between devices, from_everyone(): return lax.all_to_all(copies, axis, split_axis=0, concat_axis=0, tiled=True)  19.6 us
    all_to_all x2, starting transfers between devices, from_everyone(): return lax.all_to_all(copies, axis, split_axis=0, concat_axis=0, tiled=True)  18.6 us
    dot_general x6, matrix products, per_device(): jnp.dot(piece, matching, preferred_element_type=jnp.float32)  7.87 us
  transfers between devices with their start and end apart: 3, of which 3 were waited for; matrix products, arithmetic and copies ran while one was open for 1% of the time, Pallas kernels for 0%

commit v1 on v0

--- a/solution.py
+++ b/solution.py
@@ -6,6 +6,24 @@
 
 TERMS = 8
 LATTICE = 0.25
+
+
+def joined_along(blocks, dim):
+    shape = list(blocks.shape[1:])
+    shape[dim] *= blocks.shape[0]
+    return jnp.moveaxis(blocks, 0, dim).reshape(shape)
+
+
+def collected_by_bits(array, axis):
+    size = lax.axis_size(axis)
+    parts = array[None]
+    for level in range(size.bit_length() - 1):
+        stride = 1 << level
+        other = lax.ppermute(parts, axis, [(i, i ^ stride) for i in range(size)])
+        both = jnp.stack([parts, other])
+        upper = lax.axis_index(axis) >> level & 1
+        parts = jnp.where(upper == 0, both, both[::-1]).reshape(-1, *array.shape)
+    return parts
 
 
 def from_everyone(shard, axis):
@@ -80,7 +98,7 @@
     mirrored = lax.all_to_all(local_sum, ("row", "col"), split_axis=1, concat_axis=0, tiled=True).T
     operator_rows = sum_at_owner(local_sum - mirrored, "depth", 1) * factor
     operator_piece = operator_rows.astype(jnp.bfloat16)
-    operator_cols = lax.all_gather(operator_piece, ("row", "col"), axis=0, tiled=True)
+    operator_cols = joined_along(collected_by_bits(operator_piece, ("row", "col")), 0)
     accum = lax.dynamic_slice_in_dim(rotation, layer_index * slab_cols, slab_cols, 1).astype(
         jnp.float32
     )

time: 355 us -> 444 us (1.25)
  the two profiles are of different devices: /device:TPU:8 before, /device:TPU:2 now
where the time goes in v1:
time: 444 us; the launch traced here: 443 us
  blocking collectives  184 us (41%)
  waiting for transfers between devices  179 us (40%)
  starting transfers between devices  38.4 us (9%)
  local copies, waits for them, and re-layouts  18.5 us (4%)
  other arithmetic  12.8 us (3%)
  matrix products  8.84 us (2%)
    ppermute x6, waiting for transfers between devices, collected_by_bits(): other = lax.ppermute(parts, axis, [(i, i ^ stride) for i in range(size)])  159 us
    all_to_all x6, blocking collectives, from_everyone(): return lax.all_to_all(copies, axis, split_axis=0, concat_axis=0, tiled=True)  120 us
    all_to_all x1, blocking collectives, per_device(): lax.all_to_all(local_sum, ('row', 'col'), split_axis=1, concat_axis=0, ti...  34.5 us
    all_to_all x1, blocking collectives, sum_at_owner(): lax.all_to_all(parts, axis, split_axis=0, concat_axis=0, tiled=True)  30.1 us
    ppermute x6, starting transfers between devices, collected_by_bits(): other = lax.ppermute(parts, axis, [(i, i ^ stride) for i in range(size)])  21.1 us
    all_to_all x2, waiting for transfers between devices, from_everyone(): return lax.all_to_all(copies, axis, split_axis=0, concat_axis=0, tiled=True)  20.1 us
    all_to_all x2, starting transfers between devices, from_everyone(): return lax.all_to_all(copies, axis, split_axis=0, concat_axis=0, tiled=True)  17.4 us
  transfers between devices with their start and end apart: 8, of which 8 were waited for; matrix products, arithmetic and copies ran while one was open for 0% of the time, Pallas kernels for 0%

profile of v1, /device:TPU:2, one launch (start us, length us, event | category | flops | bytes accessed | tf_op | source)
XLA Modules:
  0.0 443.4 jit_solution(11822035221695719354)
XLA Ops:
  0.0 0.9 dynamic-slice_bitcast_fusion
  0.9 0.9 gather_fusion.1
  1.8 0.9 gather_fusion
  2.7 0.6 broadcast_in_dim.35
  3.3 13.9 %all-to-all-start = ((bf16[64,1,2,64]{3,2,1,0:T(2,128)(2,1)}), bf16[64,1,2,64]{3,2,1,0:T(2,128)(2,1)S(1)}, u32[]{:S(2)}, u32[]{:S(2)}) async-start(bf16[64,1,2,64]{3,2,1,0:T(2,128)(2,1)} %broadcast_in_dim.35), calls=%async_computation | async-start | bytes 65536 | tf_op jit(solution)/shard_map/all_to_all | solution.py:31
  17.2 1.3 dynamic_slice.16
  19.1 0.9 multiply_reduce_fusion.1
  20.0 5.8 %all-to-all-done = bf16[64,1,2,64]{3,2,1,0:T(2,128)(2,1)S(1)} async-done(((bf16[64,1,2,64]{3,2,1,0:T(2,128)(2,1)}), bf16[64,1,2,64]{3,2,1,0:T(2,128)(2,1)S(1)}, u32[]{:S(2)}, u32[]{:S(2)}) %all-to-all-start) | async-done | bytes 16416 | tf_op jit(solution)/shard_map/all_to_all | solution.py:31
  26.3 24.1 %all_to_all.64 = f32[8,3,4096]{2,1,0:T(4,128)S(1)} all-to-all(f32[8,3,4096]{2,1,0:T(4,128)S(1)} %broadcast_in_dim.36), channel_id=1, replica_groups=mesh['row'=16,'col'=4,'depth'=8] {'depth'}, dimensions={0} | all-to-all | bytes 786432 | tf_op jit(solution)/shard_map/all_to_all | solution.py:31
  50.8 1.0 fusion.11
  51.8 2.2 all_to_all.43
  54.0 2.8 copy.62
  56.8 2.3 reshape.161
  59.1 34.5 %all_to_all.65 = f32[64,1,4096]{2,1,0:T(1,128)S(1)} all-to-all(f32[64,1,4096]{2,1,0:T(1,128)} %reshape.161), channel_id=1, replica_groups=mesh['row'=16,'col'=4,'depth'=8] {'row','col'}, dimensions={0} | all-to-all | bytes 2097152 | tf_op jit(solution)/shard_map/all_to_all | solution.py:98
  94.1 4.4 reduce.4
  98.5 2.0 reshape.162
  100.5 1.6 copy.44
  102.1 1.3 bitcast_subtract_fusion
  104.6 30.1 %all_to_all.66 = f32[8,64,512]{2,1,0:T(8,128)S(1)} all-to-all(f32[8,64,512]{2,1,0:T(8,128)S(1)} %copy.45), channel_id=1, replica_groups=mesh['row'=16,'col'=4,'depth'=8] {'depth'}, dimensions={0} | all-to-all | bytes 2097152 | tf_op jit(solution)/shard_map/all_to_all | solution.py:57
  134.8 3.0 collective-permute-start
  137.8 3.2 collective-permute-done
  141.0 4.2 collective-permute-start.1
  145.3 4.1 collective-permute-done.1
  149.5 1.9 collective-permute-start.2
  151.4 1.5 collective-permute-done.2
  153.1 3.6 collective-permute-start.3
  156.6 12.3 %collective-permute-done.3 = bf16[8,64,512]{2,1,0:T(8,128)(2,1)S(1)} collective-permute-done((bf16[8,64,512]{2,1,0:T(8,128)(2,1)S(1)}, bf16[8,64,512]{2,1,0:T(8,128)(2,1)S(1)}, u32[]{:S(2)}, u32[]{:S(2)}) %collective-permute-start.3) | collective-permute-done | bytes 524320 | tf_op jit(solution)/shard_map/ppermute | solution.py:22
  169.2 3.7 collective-permute-start.4
  172.9 45.9 %collective-permute-done.4 = bf16[16,64,512]{2,1,0:T(8,128)(2,1)S(1)} collective-permute-done((bf16[16,64,512]{2,1,0:T(8,128)(2,1)S(1)}, bf16[16,64,512]{2,1,0:T(8,128)(2,1)S(1)}, u32[]{:S(2)}, u32[]{:S(2)}) %collective-permute-start.4) | collective-permute-done | bytes 1048608 | tf_op jit(solution)/shard_map/ppermute | solution.py:22
  219.6 4.7 %collective-permute-start.5 = (bf16[32,64,512]{2,1,0:T(8,128)(2,1)S(1)}, bf16[32,64,512]{2,1,0:T(8,128)(2,1)}, u32[]{:S(2)}, u32[]{:S(2)}) collective-permute-start(bf16[32,64,512]{2,1,0:T(8,128)(2,1)S(1)} %bitcast.107), channel_id=1, source_target_pairs={{0,256},{8,264},{16,272},{24,280},{32,288},{40,296},{48,304},{56,3... | collective-permute-start | bytes 6291464 | tf_op jit(solution)/shard_map/ppermute | solution.py:22
  224.3 92.2 %collective-permute-done.5 = bf16[32,64,512]{2,1,0:T(8,128)(2,1)} collective-permute-done((bf16[32,64,512]{2,1,0:T(8,128)(2,1)S(1)}, bf16[32,64,512]{2,1,0:T(8,128)(2,1)}, u32[]{:S(2)}, u32[]{:S(2)}) %collective-permute-start.5) | collective-permute-done | bytes 2097184 | tf_op jit(solution)/shard_map/ppermute | solution.py:22
  316.6 2.0 pad_maximum_fusion
  318.6 1.2 reverse_select_fusion
  319.8 0.8 fusion.8
  320.7 20.4 %all_to_all.67 = bf16[8,64,512]{2,1,0:T(8,128)(2,1)S(1)} all-to-all(bf16[8,64,512]{2,1,0:T(8,128)(2,1)S(1)} %broadcast_in_dim.37), channel_id=1, replica_groups=mesh['row'=16,'col'=4,'depth'=8] {'depth'}, dimensions={0} | all-to-all | bytes 1048576 | tf_op jit(solution)/shard_map/all_to_all | solution.py:31
  341.1 0.8 fusion
  342.0 20.2 %all_to_all.68 = bf16[8,64,512]{2,1,0:T(8,128)(2,1)S(1)} all-to-all(bf16[8,64,512]{2,1,0:T(8,128)(2,1)S(1)} %broadcast_in_dim.38), channel_id=1, replica_groups=mesh['row'=16,'col'=4,'depth'=8] {'depth'}, dimensions={0} | all-to-all | bytes 1048576 | tf_op jit(solution)/shard_map/all_to_all | solution.py:31
  362.3 0.8 fusion.1
  363.1 19.3 %all_to_all.69 = bf16[8,64,512]{2,1,0:T(8,128)(2,1)S(1)} all-to-all(bf16[8,64,512]{2,1,0:T(8,128)(2,1)S(1)} %broadcast_in_dim.39), channel_id=1, replica_groups=mesh['row'=16,'col'=4,'depth'=8] {'depth'}, dimensions={0} | all-to-all | bytes 1048576 | tf_op jit(solution)/shard_map/all_to_all | solution.py:31
  382.4 0.8 fusion.2
  383.3 18.2 %all_to_all.70 = bf16[8,64,512]{2,1,0:T(8,128)(2,1)S(1)} all-to-all(bf16[8,64,512]{2,1,0:T(8,128)(2,1)S(1)} %broadcast_in_dim.40), channel_id=1, replica_groups=mesh['row'=16,'col'=4,'depth'=8] {'depth'}, dimensions={0} | all-to-all | bytes 1048576 | tf_op jit(solution)/shard_map/all_to_all | solution.py:31
  401.6 0.8 fusion.3
  402.5 17.6 %all_to_all.71 = bf16[8,64,512]{2,1,0:T(8,128)(2,1)S(1)} all-to-all(bf16[8,64,512]{2,1,0:T(8,128)(2,1)S(1)} %broadcast_in_dim.41), channel_id=1, replica_groups=mesh['row'=16,'col'=4,'depth'=8] {'depth'}, dimensions={0} | all-to-all | bytes 1048576 | tf_op jit(solution)/shard_map/all_to_all | solution.py:31
  420.2 0.8 fusion.4
  421.0 0.9 broadcast_in_dim.42
  421.9 3.5 all-to-all-start.9
  425.4 14.3 %all-to-all-done.9 = bf16[8,64,512]{2,1,0:T(8,128)(2,1)S(1)} async-done(((bf16[8,64,512]{2,1,0:T(8,128)(2,1)}), bf16[8,64,512]{2,1,0:T(8,128)(2,1)S(1)}, u32[]{:S(2)}, u32[]{:S(2)}) %all-to-all-start.9) | async-done | bytes 524320 | tf_op jit(solution)/shard_map/all_to_all | solution.py:31
  439.7 3.7 fusion.7
  (45 shorter events, 4.4 us)
Async XLA Ops:
  0.0 50.8 %copy-start.3 = (bf16[1,64,4096]{2,1,0:T(8,128)(2,1)S(1)}, bf16[1,64,4096]{2,1,0:T(8,128)(2,1)}, u32[]{:S(2)}) copy-start(bf16[1,64,4096]{2,1,0:T(8,128)(2,1)} %param.6) | copy-start | bytes 1572868
  0.0 50.8 %copy-start.2 = (bf16[1,64,4096]{2,1,0:T(8,128)(2,1)S(1)}, bf16[1,64,4096]{2,1,0:T(8,128)(2,1)}, u32[]{:S(2)}) copy-start(bf16[1,64,4096]{2,1,0:T(8,128)(2,1)} %param.5) | copy-start | bytes 1572868
  3.3 22.5 %all-to-all-start = ((bf16[64,1,2,64]{3,2,1,0:T(2,128)(2,1)}), bf16[64,1,2,64]{3,2,1,0:T(2,128)(2,1)S(1)}, u32[]{:S(2)}, u32[]{:S(2)}) async-start(bf16[64,1,2,64]{3,2,1,0:T(2,128)(2,1)} %broadcast_in_dim.35), calls=%async_computation | async-start | bytes 65536 | tf_op jit(solution)/shard_map/all_to_all | solution.py:31
  134.8 6.2 %collective-permute-start = (bf16[1,64,512]{2,1,0:T(8,128)(2,1)S(1)}, bf16[1,64,512]{2,1,0:T(8,128)(2,1)S(1)}, u32[]{:S(2)}, u32[]{:S(2)}) collective-permute-start(bf16[1,64,512]{2,1,0:T(8,128)(2,1)S(1)} %get-tuple-element.10), channel_id=1, source_target_pairs={{0,8},{8,0},{16,24},{24,16},{32,40},{40,32},{48,56},{56,48},{64,72... | collective-permute-start | bytes 196616 | tf_op jit(solution)/shard_map/ppermute | solution.py:22
  141.0 8.4 %collective-permute-start.1 = (bf16[2,64,512]{2,1,0:T(8,128)(2,1)S(1)}, bf16[2,64,512]{2,1,0:T(8,128)(2,1)S(1)}, u32[]{:S(2)}, u32[]{:S(2)}) collective-permute-start(bf16[2,64,512]{2,1,0:T(8,128)(2,1)S(1)} %get-tuple-element.8), channel_id=1, source_target_pairs={{0,16},{8,24},{16,0},{24,8},{32,48},{40,56},{48,32},{56,40},{64,80... | collective-permute-start | bytes 393224 | tf_op jit(solution)/shard_map/ppermute | solution.py:22
  149.5 3.4 collective-permute-start.2
  153.1 15.9 %collective-permute-start.3 = (bf16[8,64,512]{2,1,0:T(8,128)(2,1)S(1)}, bf16[8,64,512]{2,1,0:T(8,128)(2,1)S(1)}, u32[]{:S(2)}, u32[]{:S(2)}) collective-permute-start(bf16[8,64,512]{2,1,0:T(8,128)(2,1)S(1)} %bitcast.124), channel_id=1, source_target_pairs={{0,64},{8,72},{16,80},{24,88},{32,96},{40,104},{48,112},{56,120},{... | collective-permute-start | bytes 1572872 | tf_op jit(solution)/shard_map/ppermute | solution.py:22
  169.2 49.6 %collective-permute-start.4 = (bf16[16,64,512]{2,1,0:T(8,128)(2,1)S(1)}, bf16[16,64,512]{2,1,0:T(8,128)(2,1)S(1)}, u32[]{:S(2)}, u32[]{:S(2)}) collective-permute-start(bf16[16,64,512]{2,1,0:T(8,128)(2,1)S(1)} %bitcast.111), channel_id=1, source_target_pairs={{0,128},{8,136},{16,144},{24,152},{32,160},{40,168},{48,176},{56,1... | collective-permute-start | bytes 3145736 | tf_op jit(solution)/shard_map/ppermute | solution.py:22
  219.6 97.0 %collective-permute-start.5 = (bf16[32,64,512]{2,1,0:T(8,128)(2,1)S(1)}, bf16[32,64,512]{2,1,0:T(8,128)(2,1)}, u32[]{:S(2)}, u32[]{:S(2)}) collective-permute-start(bf16[32,64,512]{2,1,0:T(8,128)(2,1)S(1)} %bitcast.107), channel_id=1, source_target_pairs={{0,256},{8,264},{16,272},{24,280},{32,288},{40,296},{48,304},{56,3... | collective-permute-start | bytes 6291464 | tf_op jit(solution)/shard_map/ppermute | solution.py:22
  318.6 1.2 copy-start.1
  319.8 100.4 %copy-start = (bf16[2,32,64,512]{3,2,1,0:T(8,128)(2,1)}, bf16[2,32,64,512]{3,2,1,0:T(8,128)(2,1)S(1)}, u32[]{:S(2)}) copy-start(bf16[2,32,64,512]{3,2,1,0:T(8,128)(2,1)S(1)} %reverse_select_fusion) | copy-start | bytes 12582916
  421.9 17.8 %all-to-all-start.9 = ((bf16[8,64,512]{2,1,0:T(8,128)(2,1)}), bf16[8,64,512]{2,1,0:T(8,128)(2,1)S(1)}, u32[]{:S(2)}, u32[]{:S(2)}) async-start(bf16[8,64,512]{2,1,0:T(8,128)(2,1)} %broadcast_in_dim.42), calls=%async_computation.9 | async-start | bytes 1048576 | tf_op jit(solution)/shard_map/all_to_all | solution.py:31
